TPU v7x, 32 devices: a whole 2x2x4 slice. The times are simulated.
32 devices in a mesh: rel: 4 (over x, core), dst: 4 (over z), mp: 2 (over y).
Axes of the slice: x: 2, y: 2, z: 4, core: 2. Of those that a mesh axis runs over, the one named last changes fastest.
Arguments:
- node_table: bfloat16 [16384, 512], P(('rel', 'dst')), may hold values from -6 to 6
- edge_weights: bfloat16 [4, 32, 128, 128], P('rel', 'dst'), may hold values from -0.5 to 0.5
- src_ids: int32 [4, 32, 128], P('rel', 'dst'), may hold values from 0 to 1023
- dst_ids: int32 [4, 32, 128], P('rel', 'dst'), may hold values from 0 to 511
- block_mask: int32 [4, 32], P('rel', 'dst'), may hold values 0 or 1
- basis_coef: float32 [4, 32], P('rel'), may hold values from -0.375 to 0.375
- basis_mats: bfloat16 [32, 512, 512], P(None, None, 'mp'), may hold values from -0.25 to 0.25
- type_bias: float32 [4, 512], P(None, 'mp'), may hold values from -3 to 3
- type_rows: int32 [4], replicated, may hold values from 1 to 256, 512 in all
- cotangent: bfloat16 [2048, 512], P(('rel', 'dst'), 'mp'), may hold values from -0.005859375 to 0.005859375
Outputs:
- layer_out: bfloat16 [2048, 512], P(('rel', 'dst'), 'mp')
- coef_grad: float32 [4, 32], P('rel')
Inputs may be any that keep to these rules, and one draw needn't show every extreme that they name: `type_rows`: the 4 counts sum to 512.
All inputs are finite; a program needn't handle non-finite values. No bound on the sum of `block_mask` on one device may be relied on, other than what follows from the above.
Results may differ from a plain program's by a relative error of at most 0.0062.
Values may be sent and summed in bfloat16 or wider, within the bound.
No kernel may reach another device: no remote copies, remote signals or barrier semaphores. Data moves between devices by JAX's collectives and lax.ppermute only.
A program may use at most 64 MiB of HBM per device.

v0:
```python
import jax
import jax.numpy as jnp
from jax import lax
from jax.sharding import PartitionSpec as P

highest = lax.Precision.HIGHEST


def on_device(
    node_table,
    edge_weights,
    src_ids,
    dst_ids,
    block_mask,
    basis_coef,
    basis_mats,
    type_bias,
    type_rows,
    cotangent,
):
    features = node_table.shape[1]
    out_cols = basis_mats.shape[2]
    basis_count = basis_mats.shape[0]
    block_count = edge_weights.shape[1]
    block_rows = edge_weights.shape[2]
    local_rows = cotangent.shape[0]
    owner_span = local_rows * lax.axis_size("rel")
    contract_rows = (((0,), (0,)), ((), ()))
    picked = jnp.take(node_table, src_ids[0].reshape(-1), axis=0).reshape(
        block_count, block_rows, features
    )
    scaled = edge_weights[0] * block_mask[0][:, None, None].astype(jnp.bfloat16)
    messages = jnp.einsum(
        "kij,kjf->kif", scaled, picked, preferred_element_type=jnp.float32
    ).astype(jnp.bfloat16)
    basis_flat = basis_mats.reshape(basis_count, -1)
    mixing = jnp.dot(basis_coef[0], basis_flat, precision=highest)
    weight = mixing.reshape(features, out_cols).astype(jnp.bfloat16)
    owner_grad = lax.all_gather(cotangent, "rel", axis=0, tiled=True)
    slot_local = dst_ids[0]
    arrived, arrived_ids = (
        lax.all_to_all(messages, "dst", split_axis=0, concat_axis=0, tiled=True),
        lax.all_to_all(slot_local, "dst", split_axis=0, concat_axis=0, tiled=True),
    )
    flat_rows = arrived.reshape(-1, features)
    outgoing = jnp.dot(flat_rows, weight, preferred_element_type=jnp.float32).astype(jnp.bfloat16)
    selector = (
        jnp.arange(owner_span, dtype=jnp.int32)[:, None] == arrived_ids.reshape(1, -1)
    ).astype(jnp.bfloat16)
    summed = jnp.dot(selector, outgoing, preferred_element_type=jnp.float32)
    wanted = lax.dot_general(
        selector, owner_grad, contract_rows, preferred_element_type=jnp.float32
    ).astype(jnp.bfloat16)
    outer_sum = lax.dot_general(
        flat_rows, wanted, contract_rows, preferred_element_type=jnp.float32
    )
    relation_total = lax.psum_scatter(summed, "rel", scatter_dimension=0, tiled=True)
    position = lax.axis_index("rel") * local_rows + jnp.arange(local_rows, dtype=jnp.int32)
    bounds = jnp.cumsum(type_rows)
    row_kind = jnp.sum((position[:, None] >= bounds[None, :]).astype(jnp.int32), axis=1)
    kind_table = (
        row_kind[:, None] == jnp.arange(type_rows.shape[0], dtype=jnp.int32)[None, :]
    ).astype(jnp.float32)
    row_bias = jnp.dot(kind_table, type_bias, precision=highest)
    layer_out = (relation_total + row_bias).astype(jnp.bfloat16)
    partial_value = jnp.dot(basis_flat, outer_sum.reshape(-1), precision=highest)
    basis_grads = lax.psum(partial_value, ("dst", "mp"))
    return (layer_out, basis_grads[None, :])


def solution(mesh):
    in_specs = (
        P(("rel", "dst"), None),
        P("rel", "dst", None, None),
        P("rel", "dst", None),
        P("rel", "dst", None),
        P("rel", "dst"),
        P("rel", None),
        P(None, None, "mp"),
        P(None, "mp"),
        P(),
        P(("rel", "dst"), "mp"),
    )
    out_specs = (P(("rel", "dst"), "mp"), P("rel", None))
    return jax.shard_map(
        on_device, mesh=mesh, in_specs=in_specs, out_specs=out_specs, check_vma=False
    )
```

profile of v0, /device:TPU:0, one launch (start us, length us, event | category | flops | bytes accessed | tf_op | source)
XLA Modules:
  0.0 98.5 jit_solution(5001905134119328474)
XLA Ops:
  7.2 0.0 copy-start
  7.2 0.0 copy-start.1
  7.2 0.0 copy-start.2
  7.2 0.0 copy-start.4
  7.2 6.5 %all-to-all-start = ((s32[4,2,128]{2,1,0:T(2,128)}), s32[4,2,128]{2,1,0:T(2,128)S(1)}, u32[]{:S(2)}, u32[]{:S(2)}) async-start(s32[4,2,128]{2,1,0:T(2,128)} %bitcast.52), calls=%async_computation | async-start | bytes 8192 | tf_op jit(solution)/shard_map/all_to_all | solution.py:43
  13.7 0.7 compare_and_fusion
  14.4 0.7 compare_select_fusion
  15.1 0.7 convert_bitcast_fusion
  15.8 0.0 copy-done
  15.8 4.0 %gather_fusion = bf16[1024,512]{1,0:T(8,128)(2,1)S(1)} fusion(bf16[1024,512]{1,0:T(8,128)(2,1)S(1)} %copy-done, s32[1024]{0:T(1024)S(1)} %broadcast_clamp_fusion), kind=kCustom, calls=%fused_computation | custom fusion | bytes 2101248 | tf_op jit(solution)/shard_map/jit(_take)/gather | solution.py:29
  19.7 1.5 %convolution_convert_fusion = bf16[8,128,512]{2,1,0:T(8,128)(2,1)} fusion(bf16[8,128,512]{2,1,0:T(8,128)(2,1)S(1)} %bitcast.47, pred[8,128]{1,0:T(8,128)(4,1)S(1)} %compare_and_fusion, bf16[1,8,128,128]{3,2,1,0:T(8,128)(2,1)S(1)} %copy-done.1, bf16[8]{0:T(256)(128)(2,1)S(1)} %convert_bitcast_fusion), kind=kOutput, calls=%fused_computation.9 | convolution fusion | flops 135397376 | bytes 2360336 | tf_op jit(solution)/shard_map/kij,kjf->kif/dot_general | solution.py:33
  21.2 0.0 all-to-all-done
  21.2 5.1 %all-to-all-start.1 = ((bf16[8,128,512]{2,1,0:T(8,128)(2,1)}), bf16[8,128,512]{2,1,0:T(8,128)(2,1)S(1)}, u32[]{:S(2)}, u32[]{:S(2)}) async-start(bf16[8,128,512]{2,1,0:T(8,128)(2,1)} %convolution_convert_fusion), calls=%async_computation.1 | async-start | bytes 2097152 | tf_op jit(solution)/shard_map/all_to_all | solution.py:42
  26.3 5.8 %all_gather.3 = bf16[512,256]{1,0:T(8,128)(2,1)S(1)} all-gather(bf16[128,256]{1,0:T(8,128)(2,1)S(1)} %copy-done.2), channel_id=1, replica_groups=mesh['rel'=4,'dst'=4,'mp'=2] {'rel'}, dimensions={0}, use_global_device_ids=true | all-gather | bytes 327680 | tf_op jit(solution)/shard_map/all_gather | solution.py:39
  32.1 11.5 %fusion = bf16[1,512,256]{2,0,1:T(2,128)(2,1)S(1)} fusion(f32[1,32]{1,0:T(1,128)S(1)} %copy-done.4, bf16[4,8,512,256]{3,2,1,0:T(8,128)(2,1)} %bitcast.55), kind=kOutput, calls=%fused_computation.1 | convolution fusion | flops 50331648 | bytes 8650880 | tf_op jit(solution)/shard_map/dot_general | solution.py:37
  43.6 7.9 %all-to-all-done.1 = bf16[8,128,512]{2,1,0:T(8,128)(2,1)S(1)} async-done(((bf16[8,128,512]{2,1,0:T(8,128)(2,1)}), bf16[8,128,512]{2,1,0:T(8,128)(2,1)S(1)}, u32[]{:S(2)}, u32[]{:S(2)}) %all-to-all-start.1) | async-done | bytes 1048608 | tf_op jit(solution)/shard_map/all_to_all | solution.py:42
  51.5 1.9 %fusion.6 = f32[512,256]{1,0:T(8,128)} fusion(bf16[1024,512]{1,0:T(8,128)(2,1)S(1)} %bitcast.48, s32[1024]{0:T(1024)S(1)} %bitcast.53, bf16[1,512,256]{2,0,1:T(2,128)(2,1)S(1)} %fusion), kind=kOutput, calls=%fused_computation.8 | convolution fusion | flops 537657344 | bytes 1839104 | tf_op jit(solution)/shard_map/dot_general | solution.py:50
  53.4 0.0 reduce-scatter.2.cloned.1.call-update
  53.4 0.2 reduce-window.8
  53.6 0.1 convert_reduce_fusion
  53.7 1.2 %fusion.9 = f32[512,256,1]{1,0,2:T(8,128)S(1)} fusion(bf16[1024,512]{1,0:T(8,128)(2,1)S(1)} %bitcast.49, bf16[512,256]{1,0:T(8,128)(2,1)S(1)} %all_gather.3, s32[1024]{0:T(1024)S(1)} %bitcast.54), kind=kOutput, calls=%fused_computation.13 | convolution fusion | flops 537657344 | bytes 1839104 | tf_op jit(solution)/shard_map/dot_general | solution.py:54
  54.9 14.9 %fusion.11 = f32[1,32]{1,0:T(1,128)S(1)} fusion(bf16[32,512,256]{2,1,0:T(8,128)(2,1)} %param.16, f32[512,256,1]{1,0,2:T(8,128)S(1)} %fusion.9), kind=kOutput, calls=%fused_computation.16 | convolution fusion | flops 50331648 | bytes 8913024 | tf_op jit(solution)/shard_map/dot_general | solution.py:66
  69.8 20.0 %psum.7 = f32[1,32]{1,0:T(1,128)} all-reduce(f32[1,32]{1,0:T(1,128)S(1)} %fusion.11), channel_id=1, replica_groups=mesh['rel'=4,'dst'=4,'mp'=2] {'dst','mp'}, use_global_device_ids=true, to_apply=%region_3.4 | all-reduce | flops 32 | bytes 256 | tf_op jit(solution)/shard_map/psum | solution.py:67
  89.9 1.8 %fusion.10 = bf16[128,256]{1,0:T(8,128)(2,1)} fusion(f32[128,256]{1,0:T(8,128)} %reduce-scatter.2.cloned.1.call-done, f32[4,256]{1,0:T(4,128)S(1)} %copy-done.3, s32[128]{0:T(128)S(1)} %convert_reduce_fusion), kind=kOutput, calls=%fused_computation.15 | convolution fusion | flops 1638912 | bytes 201216 | tf_op jit(solution)/shard_map/dot_general | solution.py:64
  (11 shorter events, 0.0 us)
Async XLA Ops:
  7.2 8.6 %copy-start = (bf16[1024,512]{1,0:T(8,128)(2,1)S(1)}, bf16[1024,512]{1,0:T(8,128)(2,1)}, u32[]{:S(2)}) copy-start(bf16[1024,512]{1,0:T(8,128)(2,1)} %param.10) | copy-start | bytes 3145732
  7.2 12.5 %copy-start.1 = (bf16[1,8,128,128]{3,2,1,0:T(8,128)(2,1)S(1)}, bf16[1,8,128,128]{3,2,1,0:T(8,128)(2,1)}, u32[]{:S(2)}) copy-start(bf16[1,8,128,128]{3,2,1,0:T(8,128)(2,1)} %param.11) | copy-start | bytes 786436
  7.2 19.1 %copy-start.2 = (bf16[128,256]{1,0:T(8,128)(2,1)S(1)}, bf16[128,256]{1,0:T(8,128)(2,1)}, u32[]{:S(2)}) copy-start(bf16[128,256]{1,0:T(8,128)(2,1)} %param.19) | copy-start | bytes 196612
  7.2 24.9 %copy-start.4 = (f32[1,32]{1,0:T(1,128)S(1)}, f32[1,32]{1,0:T(1,128)}, u32[]{:S(2)}) copy-start(f32[1,32]{1,0:T(1,128)} %param.15) | copy-start | bytes 388
  7.2 14.0 %all-to-all-start = ((s32[4,2,128]{2,1,0:T(2,128)}), s32[4,2,128]{2,1,0:T(2,128)S(1)}, u32[]{:S(2)}, u32[]{:S(2)}) async-start(s32[4,2,128]{2,1,0:T(2,128)} %bitcast.52), calls=%async_computation | async-start | bytes 8192 | tf_op jit(solution)/shard_map/all_to_all | solution.py:43
  21.2 30.3 %all-to-all-start.1 = ((bf16[8,128,512]{2,1,0:T(8,128)(2,1)}), bf16[8,128,512]{2,1,0:T(8,128)(2,1)S(1)}, u32[]{:S(2)}, u32[]{:S(2)}) async-start(bf16[8,128,512]{2,1,0:T(8,128)(2,1)} %convolution_convert_fusion), calls=%async_computation.1 | async-start | bytes 2097152 | tf_op jit(solution)/shard_map/all_to_all | solution.py:42
  26.3 27.1 %copy-start.5 = (s32[4]{0:T(128)S(1)}, s32[4]{0:T(128)}, u32[]{:S(2)}) copy-start(s32[4]{0:T(128)} %param.18) | copy-start | bytes 52
  26.3 63.6 %reduce-scatter.2.cloned.1.call-start = ((), (), s32[]{:S(2)}) async-start(), calls=%async_computation.3 | async-start | bytes 655360 | tf_op jit(solution)/shard_map/reduce_scatter | solution.py:57
  51.5 38.4 %copy-start.3 = (f32[4,256]{1,0:T(4,128)S(1)}, f32[4,256]{1,0:T(4,128)}, u32[]{:S(2)}) copy-start(f32[4,256]{1,0:T(4,128)} %param.17) | copy-start | bytes 12292
Sparse Core Ops, SparseCore 0:
  53.5 20.7 reduce-scatter.1
where the time goes:
time: 98.9 us; the launch traced here: 98.5 us
  matrix products  32.8 us (33%)
  blocking collectives  25.8 us (26%)
  between operations  14.1 us (14%)
  starting transfers between devices  11.6 us (12%)
  waiting for transfers between devices  7.93 us (8%)
  local copies, waits for them, and re-layouts  3.99 us (4%)
  other arithmetic  2.32 us (2%)
    psum x1, blocking collectives, on_device(): basis_grads = lax.psum(partial_value, ('dst', 'mp'))  20 us
    dot_general x1, matrix products, on_device(): jnp.dot(basis_flat, outer_sum.reshape(-1), precision=highest)  14.9 us
    dot_general x1, matrix products, on_device(): mixing = jnp.dot(basis_coef[0], basis_flat, precision=highest)  11.5 us
    all_to_all x1, waiting for transfers between devices, on_device(): lax.all_to_all(messages, 'dst', split_axis=0, concat_axis=0, tiled=True)  7.91 us
    all_to_all x1, starting transfers between devices, on_device(): lax.all_to_all(slot_local, 'dst', split_axis=0, concat_axis=0, tiled=True)  6.49 us
    all_gather x1, blocking collectives, on_device(): owner_grad = lax.all_gather(cotangent, 'rel', axis=0, tiled=True)  5.78 us
    all_to_all x1, starting transfers between devices, on_device(): lax.all_to_all(messages, 'dst', split_axis=0, concat_axis=0, tiled=True)  5.09 us
    gather x1, local copies, waits for them, and re-layouts, on_device(): jnp.take(node_table, src_ids[0].reshape(-1), axis=0)  3.96 us
  transfers between devices with their start and end apart: 3, of which 1 were waited for; matrix products, arithmetic and copies ran while one was open for 36% of the time, Pallas kernels for 0%

commit v1 on v0

--- a/solution.py
+++ b/solution.py
@@ -64,7 +64,7 @@
     row_bias = jnp.dot(kind_table, type_bias, precision=highest)
     layer_out = (relation_total + row_bias).astype(jnp.bfloat16)
     partial_value = jnp.dot(basis_flat, outer_sum.reshape(-1), precision=highest)
-    basis_grads = lax.psum(partial_value, ("dst", "mp"))
+    basis_grads = lax.psum(lax.psum(partial_value, "mp"), "dst")
     return (layer_out, basis_grads[None, :])
 
 

time: 98.9 us -> 93.9 us (0.949)
  blocking collectives: 25.8 us -> 21 us
    psum x1 -> x2, blocking collectives: 20 us -> 15.2 us  [on_device(): basis_grads = lax.psum(lax.psum(partial_value, 'mp'), 'dst')]
  transfers between devices with their start and end apart: 3 -> 3, of which waited for: 1 -> 1; matrix products, arithmetic and copies ran while one was open for 36% -> 38% of each run, Pallas kernels for 0% -> 0%
where the time goes in v1:
time: 93.9 us; the launch traced here: 93.5 us
  matrix products  32.8 us (35%)
  blocking collectives  21 us (22%)
  between operations  14.1 us (15%)
  starting transfers between devices  11.6 us (12%)
  waiting for transfers between devices  7.78 us (8%)
  local copies, waits for them, and re-layouts  3.99 us (4%)
  other arithmetic  2.32 us (2%)
    psum x2, blocking collectives, on_device(): basis_grads = lax.psum(lax.psum(partial_value, 'mp'), 'dst')  15.2 us
    dot_general x1, matrix products, on_device(): jnp.dot(basis_flat, outer_sum.reshape(-1), precision=highest)  14.9 us
    dot_general x1, matrix products, on_device(): mixing = jnp.dot(basis_coef[0], basis_flat, precision=highest)  11.5 us
    all_to_all x1, waiting for transfers between devices, on_device(): lax.all_to_all(messages, 'dst', split_axis=0, concat_axis=0, tiled=True)  7.76 us
    all_to_all x1, starting transfers between devices, on_device(): lax.all_to_all(slot_local, 'dst', split_axis=0, concat_axis=0, tiled=True)  6.49 us
    all_gather x1, blocking collectives, on_device(): owner_grad = lax.all_gather(cotangent, 'rel', axis=0, tiled=True)  5.76 us
    all_to_all x1, starting transfers between devices, on_device(): lax.all_to_all(messages, 'dst', split_axis=0, concat_axis=0, tiled=True)  5.09 us
    gather x1, local copies, waits for them, and re-layouts, on_device(): jnp.take(node_table, src_ids[0].reshape(-1), axis=0)  3.96 us
  transfers between devices with their start and end apart: 3, of which 1 were waited for; matrix products, arithmetic and copies ran while one was open for 38% of the time, Pallas kernels for 0%

profile of v1, /device:TPU:0, one launch (start us, length us, event | category | flops | bytes accessed | tf_op | source)
XLA Modules:
  0.0 93.5 jit_solution(17576689547171174921)
XLA Ops:
  7.2 0.0 copy-start
  7.2 0.0 copy-start.1
  7.2 0.0 copy-start.4
  7.2 0.0 copy-start.2
  7.2 6.5 %all-to-all-start = ((s32[4,2,128]{2,1,0:T(2,128)}), s32[4,2,128]{2,1,0:T(2,128)S(1)}, u32[]{:S(2)}, u32[]{:S(2)}) async-start(s32[4,2,128]{2,1,0:T(2,128)} %bitcast.51), calls=%async_computation | async-start | bytes 8192 | tf_op jit(solution)/shard_map/all_to_all | solution.py:43
  13.7 0.7 compare_and_fusion
  14.4 0.7 compare_select_fusion
  15.1 0.7 convert_bitcast_fusion
  15.8 4.0 %gather_fusion = bf16[1024,512]{1,0:T(8,128)(2,1)S(1)} fusion(bf16[1024,512]{1,0:T(8,128)(2,1)S(1)} %copy-done, s32[1024]{0:T(1024)S(1)} %broadcast_clamp_fusion), kind=kCustom, calls=%fused_computation | custom fusion | bytes 2101248 | tf_op jit(solution)/shard_map/jit(_take)/gather | solution.py:29
  19.7 1.5 %convolution_convert_fusion = bf16[8,128,512]{2,1,0:T(8,128)(2,1)} fusion(bf16[8,128,512]{2,1,0:T(8,128)(2,1)S(1)} %bitcast.46, pred[8,128]{1,0:T(8,128)(4,1)S(1)} %compare_and_fusion, bf16[1,8,128,128]{3,2,1,0:T(8,128)(2,1)S(1)} %copy-done.1, bf16[8]{0:T(256)(128)(2,1)S(1)} %convert_bitcast_fusion), kind=kOutput, calls=%fused_computation.9 | convolution fusion | flops 135397376 | bytes 2360336 | tf_op jit(solution)/shard_map/kij,kjf->kif/dot_general | solution.py:33
  21.2 0.0 all-to-all-done
  21.2 5.1 %all-to-all-start.1 = ((bf16[8,128,512]{2,1,0:T(8,128)(2,1)}), bf16[8,128,512]{2,1,0:T(8,128)(2,1)S(1)}, u32[]{:S(2)}, u32[]{:S(2)}) async-start(bf16[8,128,512]{2,1,0:T(8,128)(2,1)} %convolution_convert_fusion), calls=%async_computation.1 | async-start | bytes 2097152 | tf_op jit(solution)/shard_map/all_to_all | solution.py:42
  26.3 0.2 reduce-window.8
  26.5 5.8 %all_gather.3 = bf16[512,256]{1,0:T(8,128)(2,1)S(1)} all-gather(bf16[128,256]{1,0:T(8,128)(2,1)S(1)} %copy-done.2), channel_id=1, replica_groups=mesh['rel'=4,'dst'=4,'mp'=2] {'rel'}, dimensions={0}, use_global_device_ids=true | all-gather | bytes 327680 | tf_op jit(solution)/shard_map/all_gather | solution.py:39
  32.3 11.5 %fusion = bf16[1,512,256]{2,0,1:T(2,128)(2,1)S(1)} fusion(f32[1,32]{1,0:T(1,128)S(1)} %copy-done.5, bf16[4,8,512,256]{3,2,1,0:T(8,128)(2,1)} %bitcast.54), kind=kOutput, calls=%fused_computation.1 | convolution fusion | flops 50331648 | bytes 8650880 | tf_op jit(solution)/shard_map/dot_general | solution.py:37
  43.7 7.8 %all-to-all-done.1 = bf16[8,128,512]{2,1,0:T(8,128)(2,1)S(1)} async-done(((bf16[8,128,512]{2,1,0:T(8,128)(2,1)}), bf16[8,128,512]{2,1,0:T(8,128)(2,1)S(1)}, u32[]{:S(2)}, u32[]{:S(2)}) %all-to-all-start.1) | async-done | bytes 1048608 | tf_op jit(solution)/shard_map/all_to_all | solution.py:42
  51.5 1.9 %fusion.6 = f32[512,256]{1,0:T(8,128)} fusion(bf16[1024,512]{1,0:T(8,128)(2,1)S(1)} %bitcast.47, s32[1024]{0:T(1024)S(1)} %bitcast.52, bf16[1,512,256]{2,0,1:T(2,128)(2,1)S(1)} %fusion), kind=kOutput, calls=%fused_computation.8 | convolution fusion | flops 537657344 | bytes 1839104 | tf_op jit(solution)/shard_map/dot_general | solution.py:50
  53.4 0.0 reduce-scatter.2.cloned.1.call-update
  53.5 0.1 convert_reduce_fusion
  53.6 1.2 %fusion.9 = f32[512,256,1]{1,0,2:T(8,128)S(1)} fusion(bf16[1024,512]{1,0:T(8,128)(2,1)S(1)} %bitcast.48, bf16[512,256]{1,0:T(8,128)(2,1)S(1)} %all_gather.3, s32[1024]{0:T(1024)S(1)} %bitcast.53), kind=kOutput, calls=%fused_computation.13 | convolution fusion | flops 537657344 | bytes 1839104 | tf_op jit(solution)/shard_map/dot_general | solution.py:54
  54.8 14.9 %fusion.11 = f32[32]{0:T(128)S(1)} fusion(bf16[32,512,256]{2,1,0:T(8,128)(2,1)} %param.16, f32[512,256,1]{1,0,2:T(8,128)S(1)} %fusion.9), kind=kOutput, calls=%fused_computation.16 | convolution fusion | flops 50331648 | bytes 8913024 | tf_op jit(solution)/shard_map/dot_general | solution.py:66
  69.7 4.9 %psum.14 = f32[32]{0:T(128)S(1)} all-reduce(f32[32]{0:T(128)S(1)} %fusion.11), channel_id=1, replica_groups=mesh['rel'=4,'dst'=4,'mp'=2] {'mp'}, use_global_device_ids=true, to_apply=%region_3.4 | all-reduce | flops 32 | bytes 256 | tf_op jit(solution)/shard_map/psum | solution.py:67
  74.6 10.3 %psum.15 = f32[1,32]{1,0:T(1,128)} all-reduce(f32[1,32]{1,0:T(1,128)S(1)} %bitcast.57), channel_id=1, replica_groups=mesh['rel'=4,'dst'=4,'mp'=2] {'dst'}, use_global_device_ids=true, to_apply=%region_4.5 | all-reduce | flops 32 | bytes 256 | tf_op jit(solution)/shard_map/psum | solution.py:67
  84.9 1.8 %fusion.10 = bf16[128,256]{1,0:T(8,128)(2,1)} fusion(f32[128,256]{1,0:T(8,128)} %reduce-scatter.2.cloned.1.call-done, f32[4,256]{1,0:T(4,128)S(1)} %copy-done.3, s32[128]{0:T(128)S(1)} %convert_reduce_fusion), kind=kOutput, calls=%fused_computation.15 | convolution fusion | flops 1638912 | bytes 201216 | tf_op jit(solution)/shard_map/dot_general | solution.py:64
  (12 shorter events, 0.0 us)
Async XLA Ops:
  7.2 8.6 %copy-start = (bf16[1024,512]{1,0:T(8,128)(2,1)S(1)}, bf16[1024,512]{1,0:T(8,128)(2,1)}, u32[]{:S(2)}) copy-start(bf16[1024,512]{1,0:T(8,128)(2,1)} %param.10) | copy-start | bytes 3145732
  7.2 12.6 %copy-start.1 = (bf16[1,8,128,128]{3,2,1,0:T(8,128)(2,1)S(1)}, bf16[1,8,128,128]{3,2,1,0:T(8,128)(2,1)}, u32[]{:S(2)}) copy-start(bf16[1,8,128,128]{3,2,1,0:T(8,128)(2,1)} %param.11) | copy-start | bytes 786436
  7.2 19.1 %copy-start.4 = (s32[4]{0:T(128)S(1)}, s32[4]{0:T(128)}, u32[]{:S(2)}) copy-start(s32[4]{0:T(128)} %param.18) | copy-start | bytes 52
  7.2 19.3 %copy-start.2 = (bf16[128,256]{1,0:T(8,128)(2,1)S(1)}, bf16[128,256]{1,0:T(8,128)(2,1)}, u32[]{:S(2)}) copy-start(bf16[128,256]{1,0:T(8,128)(2,1)} %param.19) | copy-start | bytes 196612
  7.2 25.1 %copy-start.5 = (f32[1,32]{1,0:T(1,128)S(1)}, f32[1,32]{1,0:T(1,128)}, u32[]{:S(2)}) copy-start(f32[1,32]{1,0:T(1,128)} %param.15) | copy-start | bytes 388
  7.2 14.0 %all-to-all-start = ((s32[4,2,128]{2,1,0:T(2,128)}), s32[4,2,128]{2,1,0:T(2,128)S(1)}, u32[]{:S(2)}, u32[]{:S(2)}) async-start(s32[4,2,128]{2,1,0:T(2,128)} %bitcast.51), calls=%async_computation | async-start | bytes 8192 | tf_op jit(solution)/shard_map/all_to_all | solution.py:43
  21.2 30.3 %all-to-all-start.1 = ((bf16[8,128,512]{2,1,0:T(8,128)(2,1)}), bf16[8,128,512]{2,1,0:T(8,128)(2,1)S(1)}, u32[]{:S(2)}, u32[]{:S(2)}) async-start(bf16[8,128,512]{2,1,0:T(8,128)(2,1)} %convolution_convert_fusion), calls=%async_computation.1 | async-start | bytes 2097152 | tf_op jit(solution)/shard_map/all_to_all | solution.py:42
  26.3 58.6 %reduce-scatter.2.cloned.1.call-start = ((), (), s32[]{:S(2)}) async-start(), calls=%async_computation.3 | async-start | bytes 655360 | tf_op jit(solution)/shard_map/reduce_scatter | solution.py:57
  51.5 33.4 %copy-start.3 = (f32[4,256]{1,0:T(4,128)S(1)}, f32[4,256]{1,0:T(4,128)}, u32[]{:S(2)}) copy-start(f32[4,256]{1,0:T(4,128)} %param.17) | copy-start | bytes 12292
Sparse Core Ops, SparseCore 0:
  53.6 20.7 reduce-scatter.1
